TPU v7x, 32 devices: a whole 2x2x4 slice. The times are simulated.
32 devices in a mesh: grp: 4 (over y, x), dev: 8 (over z, core).
Axes of the slice: x: 2, y: 2, z: 4, core: 2. Of those that a mesh axis runs over, the one named last changes fastest.
Arguments:
- points: bfloat16 [65536, 256], P(('grp', 'dev')), may hold values from -6 to 6
- ridge: float32 [1024], replicated, may hold values from 0.25 to 2
- landmark_ids: int32 [1024], replicated, may hold values from 0 to 65535, as said below
Outputs:
- features: bfloat16 [65536, 1024], P(('grp', 'dev'))
Inputs may be any that keep to these rules, and one draw needn't show every extreme that they name: `landmark_ids`: sorted ascending, all distinct.
All inputs are finite; a program needn't handle non-finite values.
Results may differ from a plain program's by a relative error of at most 0.0015.
Values may be sent and summed in bfloat16 or wider, within the bound.
No kernel may reach another device: no remote copies, remote signals or barrier semaphores. Data moves between devices by JAX's collectives and lax.ppermute only.
A program may use at most 128 MiB of HBM per device.

v0:
```python
import jax
import jax.numpy as jnp
from jax import lax
from jax.sharding import PartitionSpec as P


def kernel_block(left, right):
    left_sq = jnp.sum(jnp.square(left.astype(jnp.float32)), axis=1)
    right_sq = jnp.sum(jnp.square(right.astype(jnp.float32)), axis=1)
    inner = jnp.dot(left, right.T, preferred_element_type=jnp.float32)
    width = left.shape[1]
    return jnp.exp(-(left_sq[:, None] + right_sq[None, :] - 2.0 * inner) / (2.0 * width))


def shards(points, ridge, landmark_ids):
    count = points.shape[0]
    start = lax.axis_index(("grp", "dev")) * count
    offset = landmark_ids - start
    inside = (offset >= 0) & (offset < count)
    picked = points[jnp.clip(offset, 0, count - 1)]
    filled = jnp.where(inside[:, None], picked.astype(jnp.float32), 0.0)
    marks = lax.psum(filled, ("grp", "dev")).astype(jnp.bfloat16)
    core = kernel_block(marks, marks) + jnp.diag(ridge)
    lower = jnp.linalg.cholesky(core)
    cross = kernel_block(points, marks)
    raw = lax.linalg.triangular_solve(lower, cross, left_side=False, lower=True, transpose_a=True)
    total_rows = count * lax.axis_size(("grp", "dev"))
    totals, squares = lax.psum(
        (jnp.sum(raw, axis=0), jnp.sum(jnp.square(raw), axis=0)), ("grp", "dev")
    )
    mean = totals / total_rows
    var = jnp.maximum(squares / total_rows - jnp.square(mean), 0.0)
    centered = raw - mean[None, :]
    return (centered / jnp.sqrt(var + 1e-05)[None, :]).astype(jnp.bfloat16)


def solution(mesh):
    placed = (P(("grp", "dev"), None), P(), P())
    return jax.shard_map(
        shards, mesh=mesh, in_specs=placed, out_specs=P(("grp", "dev"), None), check_vma=False
    )
```

profile of v0, /device:TPU:0, one launch (start us, length us, event | category | flops | bytes accessed | tf_op | source)
XLA Modules:
  0.0 495.3 jit_solution(2860757767389505931)
XLA Ops:
  3.0 4.9 gather_fusion
  8.1 53.3 %all-reduce.3 = bf16[1024,256]{1,0:T(8,128)(2,1)S(1)} all-reduce(f32[1024,256]{1,0:T(8,128)S(1)} %convert_select_fusion), channel_id=1, replica_groups=mesh['grp'=4,'dev'=8] {'grp','dev'}, use_global_device_ids=true, to_apply=%region_1.2 | all-reduce | flops 262144 | bytes 1572864 | tf_op jit(solution)/shard_map/psum | solution.py:22
  61.6 4.3 fusion.2
  66.0 5.6 %subtract_negate_fusion = (f32[1024,1024]{0,1:T(8,128)}, f32[1024,1024]{0,1:T(8,128)}, f32[1024,1024]{0,1:T(8,128)}) fusion(f32[1024]{0:T(1024)S(1)} %multiply_reduce_fusion.2, bf16[1024,256]{1,0:T(8,128)(2,1)S(1)} %all-reduce.3), kind=kOutput, calls=%fused_computation.27 | convolution fusion | flops 541065216 | bytes 13111296 | tf_op jit(solution)/shard_map/dot_general | solution.py:10
  71.6 5.4 %copy.5 = f32[1024,1024]{1,0:T(8,128)} copy(f32[1024,1024]{0,1:T(8,128)} %get-tuple-element.76) | data formatting | bytes 8388608 | tf_op jit(solution)/shard_map/neg | solution.py:12
  76.9 5.3 %copy.6 = f32[1024,1024]{1,0:T(8,128)} copy(f32[1024,1024]{0,1:T(8,128)} %get-tuple-element.77) | data formatting | bytes 8388608 | tf_op jit(solution)/shard_map/add | solution.py:12
  82.3 6.3 %fusion.16 = f32[1024,1024]{1,0:T(8,128)S(1)} fusion(f32[1024,1024]{1,0:T(8,128)} %copy.6, f32[1024,1024]{1,0:T(8,128)} %copy.5, f32[1024,1024]{0,1:T(8,128)} %get-tuple-element.78, f32[1024]{0:T(1024)S(1)} %copy-done.5), kind=kLoop, calls=%fused_computation.24 | loop fusion | flops 13631488 | bytes 16781312 | tf_op jit(solution)/shard_map/jit(cholesky)/div | solution.py:24
  90.6 11.7 %cholesky.222 = f32[128,128]{1,0:T(8,128)S(1)} custom-call(f32[128,128]{1,0:T(8,128)S(1)} %cholesky.577), custom_call_target="Cholesky" | custom-call | tf_op jit(solution)/shard_map/jit(cholesky)/cholesky | solution.py:24
  102.4 9.8 %custom-call.62 = f32[1,128,128]{1,2,0:T(8,128)S(1)} custom-call(f32[1,128,128]{2,1,0:T(8,128)S(1)} %get-tuple-element.73), custom_call_target="InvertDiagBlocksLowerTriangular" | custom-call | tf_op jit(solution)/shard_map/jit(cholesky)/cholesky | solution.py:24
  112.2 2.5 cholesky.254
  114.7 2.3 constant_dynamic-update-slice_fusion.32
  118.6 11.7 %cholesky.243 = f32[128,128]{1,0:T(8,128)S(1)} custom-call(f32[128,128]{1,0:T(8,128)S(1)} %cholesky.581), custom_call_target="Cholesky" | custom-call | tf_op jit(solution)/shard_map/jit(cholesky)/cholesky | solution.py:24
  132.9 10.2 %custom-call.63 = f32[1,128,128]{1,2,0:T(8,128)S(1)} custom-call(f32[1,128,128]{2,1,0:T(8,128)S(1)} %get-tuple-element.70), custom_call_target="InvertDiagBlocksLowerTriangular" | custom-call | tf_op jit(solution)/shard_map/jit(cholesky)/cholesky | solution.py:24
  146.4 11.7 %cholesky.466 = f32[128,128]{1,0:T(8,128)S(1)} custom-call(f32[128,128]{1,0:T(8,128)S(1)} %cholesky.586), custom_call_target="Cholesky" | custom-call | tf_op jit(solution)/shard_map/jit(cholesky)/cholesky | solution.py:24
  160.1 9.8 %custom-call.64 = f32[1,128,128]{1,2,0:T(8,128)S(1)} custom-call(f32[1,128,128]{2,1,0:T(8,128)S(1)} %get-tuple-element.67), custom_call_target="InvertDiagBlocksLowerTriangular" | custom-call | tf_op jit(solution)/shard_map/jit(cholesky)/cholesky | solution.py:24
  171.0 2.3 convolution_subtract_fusion.7
  173.4 11.9 %cholesky.485 = f32[128,128]{1,0:T(8,128)S(1)} custom-call(f32[128,128]{1,0:T(8,128)S(1)} %cholesky.591), custom_call_target="Cholesky" | custom-call | tf_op jit(solution)/shard_map/jit(cholesky)/cholesky | solution.py:24
  187.2 9.8 %custom-call.65 = f32[1,128,128]{1,2,0:T(8,128)S(1)} custom-call(f32[1,128,128]{2,1,0:T(8,128)S(1)} %get-tuple-element.64), custom_call_target="InvertDiagBlocksLowerTriangular" | custom-call | tf_op jit(solution)/shard_map/jit(cholesky)/cholesky | solution.py:24
  198.1 2.3 convolution_subtract_fusion.8
  200.4 11.7 %cholesky.504 = f32[128,128]{1,0:T(8,128)S(1)} custom-call(f32[128,128]{1,0:T(8,128)S(1)} %cholesky.596), custom_call_target="Cholesky" | custom-call | tf_op jit(solution)/shard_map/jit(cholesky)/cholesky | solution.py:24
  214.0 9.8 %custom-call.66 = f32[1,128,128]{1,2,0:T(8,128)S(1)} custom-call(f32[1,128,128]{2,1,0:T(8,128)S(1)} %get-tuple-element.61), custom_call_target="InvertDiagBlocksLowerTriangular" | custom-call | tf_op jit(solution)/shard_map/jit(cholesky)/cholesky | solution.py:24
  224.8 2.5 convolution_subtract_fusion.9
  227.4 11.7 %cholesky.524 = f32[128,128]{1,0:T(8,128)S(1)} custom-call(f32[128,128]{1,0:T(8,128)S(1)} %cholesky.601), custom_call_target="Cholesky" | custom-call | tf_op jit(solution)/shard_map/jit(cholesky)/cholesky | solution.py:24
  241.0 9.8 %custom-call.67 = f32[1,128,128]{1,2,0:T(8,128)S(1)} custom-call(f32[1,128,128]{2,1,0:T(8,128)S(1)} %get-tuple-element.58), custom_call_target="InvertDiagBlocksLowerTriangular" | custom-call | tf_op jit(solution)/shard_map/jit(cholesky)/cholesky | solution.py:24
  253.9 11.7 %cholesky.544 = f32[128,128]{1,0:T(8,128)S(1)} custom-call(f32[128,128]{1,0:T(8,128)S(1)} %cholesky.606), custom_call_target="Cholesky" | custom-call | tf_op jit(solution)/shard_map/jit(cholesky)/cholesky | solution.py:24
  267.5 10.2 %custom-call.68 = f32[1,128,128]{1,2,0:T(8,128)S(1)} custom-call(f32[1,128,128]{2,1,0:T(8,128)S(1)} %get-tuple-element.55), custom_call_target="InvertDiagBlocksLowerTriangular" | custom-call | tf_op jit(solution)/shard_map/jit(cholesky)/cholesky | solution.py:24
  280.4 11.7 %cholesky.562 = f32[128,128]{1,0:T(8,128)S(1)} custom-call(f32[128,128]{1,0:T(8,128)S(1)} %convolution_subtract_fusion.11), custom_call_target="Cholesky" | custom-call | tf_op jit(solution)/shard_map/jit(cholesky)/cholesky | solution.py:24
  293.9 4.9 select_select_fusion
  298.8 22.5 %while.1 = (s32[]{:T(128)}, f32[1024,1024]{1,0:T(8,128)}, s32[8,2]{0,1:T(2,128)S(1)}, f32[8,128,128]{2,1,0:T(8,128)S(1)}, s32[]{:T(128)}) while((s32[]{:T(128)}, f32[1024,1024]{1,0:T(8,128)}, s32[8,2]{0,1:T(2,128)S(1)}, f32[8,128,128]{2,1,0:T(8,128)S(1)}, s32[]{:T(128)}) %tuple.61), condition=%wide.while_cond, body=%wide.while_body.sunk | while | flops 2 | bytes 131189 | solution.py:26
  299.4 2.2 bitcast_dynamic-update-slice_fusion.2
  302.2 2.2 bitcast_dynamic-update-slice_fusion.2
  305.0 2.2 bitcast_dynamic-update-slice_fusion.2
  310.6 2.2 bitcast_dynamic-update-slice_fusion.2
  313.5 2.2 bitcast_dynamic-update-slice_fusion.2
  321.2 78.8 %custom-call.69 = f32[8,128,128]{1,2,0:T(8,128)S(1)} custom-call(f32[8,128,128]{2,1,0:T(8,128)S(1)} %get-tuple-element.12), custom_call_target="InvertDiagBlocksLowerTriangular" | custom-call | tf_op jit(solution)/shard_map/triangular_solve | solution.py:26
  400.0 2.7 constant_dynamic-update-slice_fusion.17
  402.8 2.5 convolution_subtract_fusion.4
  406.6 2.3 convolution_subtract_fusion.3
  410.2 3.1 fusion.23
  413.3 2.3 constant_dynamic-update-slice_fusion.14
  415.6 5.0 %fusion.26 = f32[2048,128]{0,1:T(8,128)} fusion(f32[2048,128]{0,1:T(8,128)} %get-tuple-element.84, f32[2048,128]{0,1:T(8,128)S(1)} %get-tuple-element.83, f32[2048,128]{0,1:T(8,128)S(1)} %get-tuple-element.82, f32[2048,128]{0,1:T(8,128)S(1)} %get-tuple-element.81, f32[2048,1024]{0,1:T(8,128)S(1)} %bitcast.124, f32[1024,1024]{1,0:T(8,128)} %get-tuple-element.131), kind=kOutput, calls=%fused_computation.42 | convolution fusion | flops 1614020608 | bytes 6553600 | tf_op jit(solution)/shard_map/triangular_solve | solution.py:26
  420.6 2.4 constant_dynamic-update-slice_fusion.13
  423.0 4.3 convolution_subtract_fusion.2
  428.5 4.6 convolution_subtract_fusion
  434.2 5.8 %convolution_subtract_fusion.1 = f32[2048,128]{0,1:T(8,128)S(1)} fusion(f32[2048,896]{0,1:T(8,128)S(1)} %get-tuple-element.27, f32[2048,1024]{0,1:T(8,128)S(1)} %bitcast.124, f32[1024,1024]{1,0:T(8,128)} %get-tuple-element.131), kind=kOutput, calls=%fused_computation.38 | convolution fusion | flops 2818834432 | bytes 9895936 | tf_op jit(solution)/shard_map/triangular_solve | solution.py:26
  444.3 38.9 %all-reduce.1 = (f32[1024]{0:T(1024)S(1)}, f32[1024]{0:T(1024)S(1)}) all-reduce(f32[1024]{0:T(1024)S(1)} %get-tuple-element.14, f32[1024]{0:T(1024)S(1)} %get-tuple-element.13), channel_id=1, replica_groups=mesh['grp'=4,'dev'=8] {'grp','dev'}, use_global_device_ids=true, to_apply=%region_22.23 | all-reduce | flops 2048 | bytes 16384 | tf_op jit(solution)/shard_map/psum | solution.py:28
  483.1 5.3 %divide_convert_fusion = bf16[2048,1024]{0,1:T(8,128)(2,1)} fusion(f32[2048,1024]{0,1:T(8,128)} %copy-done, f32[1024]{0:T(1024)S(1)} %get-tuple-element.75, f32[1024]{0:T(1024)S(1)} %get-tuple-element.74), kind=kLoop, calls=%fused_computation.7 | loop fusion | flops 6291456 | bytes 12591104 | tf_op jit(solution)/shard_map/convert_element_type | solution.py:34
  488.5 6.4 %copy.7 = bf16[2048,1024]{1,0:T(8,128)(2,1)} copy(bf16[2048,1024]{0,1:T(8,128)(2,1)} %divide_convert_fusion) | data formatting | bytes 8388608 | tf_op jit(solution)/shard_map/convert_element_type | solution.py:34
  (83 shorter events, 48.7 us)
Async XLA Ops:
  3.0 58.6 %copy-start.1 = (bf16[2048,256]{1,0:T(8,128)(2,1)S(1)}, bf16[2048,256]{1,0:T(8,128)(2,1)}, u32[]{:S(2)}) copy-start(bf16[2048,256]{1,0:T(8,128)(2,1)} %param.3) | copy-start | bytes 3145732
  76.9 5.4 %copy-start.5 = (f32[1024]{0:T(1024)S(1)}, f32[1024]{0:T(1024)}, u32[]{:S(2)}) copy-start(f32[1024]{0:T(1024)} %param.4) | copy-start | bytes 12292
  88.6 2.0 copy-start.2
  400.0 5.3 %copy-start.3 = (f32[8,128,128]{1,2,0:T(8,128)}, f32[8,128,128]{1,2,0:T(8,128)S(1)}, u32[]{:S(2)}) copy-start(f32[8,128,128]{1,2,0:T(8,128)S(1)} %custom-call.69) | copy-start | bytes 1572868
  400.0 6.6 %slice-start = ((s8[8388608]{0:T(1024)(128)(4,1)}), s8[4194304]{0:T(1024)(128)(4,1)S(1)}, s32[]{:S(2)}) async-start(s8[8388608]{0:T(1024)(128)(4,1)} %bitcast.123), calls=%async_computation | async-start | bytes 8388608
  402.8 3.8 slice-start.1
  406.6 2.3 copy-start.4
  441.0 3.2 copy-start
where the time goes:
time: 502 us; the launch traced here: 495 us
  other arithmetic  272 us (54%)
  blocking collectives  92.1 us (18%)
  matrix products  74 us (15%)
  local copies, waits for them, and re-layouts  51 us (10%)
  between operations  5.8 us (1%)
    another operation x30, other arithmetic, shards(): lower = jnp.linalg.cholesky(core)  172 us
    another operation x3, other arithmetic, shards(): lax.linalg.triangular_solve(lower, cross, left_side=False, lower=True, tr...  83.7 us
    psum x1, blocking collectives, shards(): marks = lax.psum(filled, ('grp', 'dev')).astype(jnp.bfloat16)  53.3 us
    another operation x15, matrix products, shards(): lax.linalg.triangular_solve(lower, cross, left_side=False, lower=True, tr...  40.8 us
    psum x1, blocking collectives, shards(): lax.psum((jnp.sum(raw, axis=0), jnp.sum(jnp.square(raw), axis=0)), ('grp'...  38.9 us
    another operation x14, matrix products, shards(): lower = jnp.linalg.cholesky(core)  23.2 us
    another operation x24, local copies, waits for them, and re-layouts  22.3 us

commit v1 on v0

--- a/solution.py
+++ b/solution.py
@@ -19,7 +19,7 @@
     inside = (offset >= 0) & (offset < count)
     picked = points[jnp.clip(offset, 0, count - 1)]
     filled = jnp.where(inside[:, None], picked.astype(jnp.float32), 0.0)
-    marks = lax.psum(filled, ("grp", "dev")).astype(jnp.bfloat16)
+    marks = jnp.sum(lax.all_gather(filled, ("grp", "dev")), axis=0).astype(jnp.bfloat16)
     core = kernel_block(marks, marks) + jnp.diag(ridge)
     lower = jnp.linalg.cholesky(core)
     cross = kernel_block(points, marks)

time: 502 us -> 672 us (1.34)
  waiting for transfers between devices: 0 us -> 197 us
  blocking collectives: 92.1 us -> 38.4 us
  between operations: 5.8 us -> 19 us
  other arithmetic: 272 us -> 284 us
    all_gather x0 -> x1, waiting for transfers between devices: none -> 197 us  [shards(): lax.all_gather(filled, ('grp', 'dev'))]
    psum x1 -> x0, blocking collectives: 53.3 us -> none  [shards(): marks = lax.psum(filled, ('grp', 'dev')).astype(jnp.bfloat16)]
    reduce_sum x0 -> x1, other arithmetic: none -> 12 us  [shards(): jnp.sum(lax.all_gather(filled, ('grp', 'dev')), axis=0).astype(jnp.bfloat16)]
  transfers between devices with their start and end apart: 0 -> 1, of which waited for: 0 -> 1; matrix products, arithmetic and copies ran while one was open for 0% -> 0% of each run, Pallas kernels for 0% -> 0%
where the time goes in v1:
time: 672 us; the launch traced here: 663 us
  other arithmetic  284 us (42%)
  waiting for transfers between devices  197 us (29%)
  matrix products  74.6 us (11%)
  local copies, waits for them, and re-layouts  50.9 us (8%)
  blocking collectives  38.4 us (6%)
  between operations  19 us (3%)
    all_gather x1, waiting for transfers between devices, shards(): lax.all_gather(filled, ('grp', 'dev'))  197 us
    another operation x30, other arithmetic, shards(): lower = jnp.linalg.cholesky(core)  172 us
    another operation x3, other arithmetic, shards(): lax.linalg.triangular_solve(lower, cross, left_side=False, lower=True, tr...  83.5 us
    another operation x15, matrix products, shards(): lax.linalg.triangular_solve(lower, cross, left_side=False, lower=True, tr...  41 us
    psum x1, blocking collectives, shards(): lax.psum((jnp.sum(raw, axis=0), jnp.sum(jnp.square(raw), axis=0)), ('grp'...  38.4 us
    another operation x14, matrix products, shards(): lower = jnp.linalg.cholesky(core)  23.3 us
    another operation x24, local copies, waits for them, and re-layouts  22.3 us
  transfers between devices with their start and end apart: 1, of which 1 were waited for; matrix products, arithmetic and copies ran while one was open for 0% of the time, Pallas kernels for 0%

profile of v1, /device:TPU:0, one launch (start us, length us, event | category | flops | bytes accessed | tf_op | source)
XLA Modules:
  0.0 663.3 jit_solution(14990910626862469653)
XLA Ops:
  8.0 4.8 gather_fusion
  14.4 196.7 %all-gather.2.cloned.1.call-done = f32[32,1024,256]{2,1,0:T(8,128)} async-done(((f32[1,1024,256]{2,1,0:T(8,128)}), f32[32,1024,256]{2,1,0:T(8,128)}) %all-gather.2.cloned.1.call-update) | async-done | bytes 33554448 | tf_op jit(solution)/shard_map/all_gather | solution.py:22
  211.1 12.0 %reduce_sum.44 = bf16[1024,256]{1,0:T(8,128)(2,1)S(1)} reduce(f32[32,1024,256]{2,1,0:T(8,128)} %all-gather.2.cloned.1.call-done, f32[]{:T(128)} %constant.289.clone.1), dimensions={0}, to_apply=%region_1.2 | reduce | flops 8126464 | bytes 34078724 | tf_op jit(solution)/shard_map/reduce_sum | solution.py:22
  223.3 5.6 subtract_negate_fusion
  228.9 5.3 copy.13
  234.3 5.3 copy.14
  239.6 6.1 fusion.16
  247.7 11.7 %cholesky.222 = f32[128,128]{1,0:T(8,128)S(1)} custom-call(f32[128,128]{1,0:T(8,128)S(1)} %cholesky.577), custom_call_target="Cholesky" | custom-call | tf_op jit(solution)/shard_map/jit(cholesky)/cholesky | solution.py:24
  259.5 2.5 cholesky.254
  262.0 4.7 fusion.2
  266.8 9.8 %custom-call.62 = f32[1,128,128]{1,2,0:T(8,128)S(1)} custom-call(f32[1,128,128]{2,1,0:T(8,128)S(1)} %get-tuple-element.73), custom_call_target="InvertDiagBlocksLowerTriangular" | custom-call | tf_op jit(solution)/shard_map/jit(cholesky)/cholesky | solution.py:24
  276.6 2.3 constant_dynamic-update-slice_fusion.32
  280.5 11.7 %cholesky.243 = f32[128,128]{1,0:T(8,128)S(1)} custom-call(f32[128,128]{1,0:T(8,128)S(1)} %cholesky.581), custom_call_target="Cholesky" | custom-call | tf_op jit(solution)/shard_map/jit(cholesky)/cholesky | solution.py:24
  292.8 9.8 %custom-call.63 = f32[1,128,128]{1,2,0:T(8,128)S(1)} custom-call(f32[1,128,128]{2,1,0:T(8,128)S(1)} %get-tuple-element.70), custom_call_target="InvertDiagBlocksLowerTriangular" | custom-call | tf_op jit(solution)/shard_map/jit(cholesky)/cholesky | solution.py:24
  305.9 11.9 %cholesky.466 = f32[128,128]{1,0:T(8,128)S(1)} custom-call(f32[128,128]{1,0:T(8,128)S(1)} %cholesky.586), custom_call_target="Cholesky" | custom-call | tf_op jit(solution)/shard_map/jit(cholesky)/cholesky | solution.py:24
  319.1 9.8 %custom-call.64 = f32[1,128,128]{1,2,0:T(8,128)S(1)} custom-call(f32[1,128,128]{2,1,0:T(8,128)S(1)} %get-tuple-element.67), custom_call_target="InvertDiagBlocksLowerTriangular" | custom-call | tf_op jit(solution)/shard_map/jit(cholesky)/cholesky | solution.py:24
  330.1 2.3 convolution_subtract_fusion.7
  332.4 11.7 %cholesky.485 = f32[128,128]{1,0:T(8,128)S(1)} custom-call(f32[128,128]{1,0:T(8,128)S(1)} %cholesky.591), custom_call_target="Cholesky" | custom-call | tf_op jit(solution)/shard_map/jit(cholesky)/cholesky | solution.py:24
  345.5 9.8 %custom-call.65 = f32[1,128,128]{1,2,0:T(8,128)S(1)} custom-call(f32[1,128,128]{2,1,0:T(8,128)S(1)} %get-tuple-element.64), custom_call_target="InvertDiagBlocksLowerTriangular" | custom-call | tf_op jit(solution)/shard_map/jit(cholesky)/cholesky | solution.py:24
  356.6 2.3 convolution_subtract_fusion.8
  358.9 11.7 %cholesky.504 = f32[128,128]{1,0:T(8,128)S(1)} custom-call(f32[128,128]{1,0:T(8,128)S(1)} %cholesky.596), custom_call_target="Cholesky" | custom-call | tf_op jit(solution)/shard_map/jit(cholesky)/cholesky | solution.py:24
  372.0 9.8 %custom-call.66 = f32[1,128,128]{1,2,0:T(8,128)S(1)} custom-call(f32[1,128,128]{2,1,0:T(8,128)S(1)} %get-tuple-element.61), custom_call_target="InvertDiagBlocksLowerTriangular" | custom-call | tf_op jit(solution)/shard_map/jit(cholesky)/cholesky | solution.py:24
  382.8 2.3 convolution_subtract_fusion.9
  385.1 12.1 %cholesky.524 = f32[128,128]{1,0:T(8,128)S(1)} custom-call(f32[128,128]{1,0:T(8,128)S(1)} %cholesky.601), custom_call_target="Cholesky" | custom-call | tf_op jit(solution)/shard_map/jit(cholesky)/cholesky | solution.py:24
  398.6 9.8 %custom-call.67 = f32[1,128,128]{1,2,0:T(8,128)S(1)} custom-call(f32[1,128,128]{2,1,0:T(8,128)S(1)} %get-tuple-element.58), custom_call_target="InvertDiagBlocksLowerTriangular" | custom-call | tf_op jit(solution)/shard_map/jit(cholesky)/cholesky | solution.py:24
  409.3 2.2 convolution_subtract_fusion.10
  411.5 11.7 %cholesky.544 = f32[128,128]{1,0:T(8,128)S(1)} custom-call(f32[128,128]{1,0:T(8,128)S(1)} %cholesky.606), custom_call_target="Cholesky" | custom-call | tf_op jit(solution)/shard_map/jit(cholesky)/cholesky | solution.py:24
  424.6 9.8 %custom-call.68 = f32[1,128,128]{1,2,0:T(8,128)S(1)} custom-call(f32[1,128,128]{2,1,0:T(8,128)S(1)} %get-tuple-element.55), custom_call_target="InvertDiagBlocksLowerTriangular" | custom-call | tf_op jit(solution)/shard_map/jit(cholesky)/cholesky | solution.py:24
  437.0 11.9 %cholesky.562 = f32[128,128]{1,0:T(8,128)S(1)} custom-call(f32[128,128]{1,0:T(8,128)S(1)} %convolution_subtract_fusion.11), custom_call_target="Cholesky" | custom-call | tf_op jit(solution)/shard_map/jit(cholesky)/cholesky | solution.py:24
  455.8 4.9 select_select_fusion
  460.6 22.5 %while.1 = (s32[]{:T(128)}, f32[1024,1024]{1,0:T(8,128)}, s32[8,2]{0,1:T(2,128)S(1)}, f32[8,128,128]{2,1,0:T(8,128)S(1)}, s32[]{:T(128)}) while((s32[]{:T(128)}, f32[1024,1024]{1,0:T(8,128)}, s32[8,2]{0,1:T(2,128)S(1)}, f32[8,128,128]{2,1,0:T(8,128)S(1)}, s32[]{:T(128)}) %tuple.61), condition=%wide.while_cond, body=%wide.while_body.sunk | while | flops 2 | bytes 131189 | solution.py:26
  461.3 2.2 bitcast_dynamic-update-slice_fusion.2
  466.9 2.2 bitcast_dynamic-update-slice_fusion.2
  469.7 2.2 bitcast_dynamic-update-slice_fusion.2
  483.1 78.6 %custom-call.69 = f32[8,128,128]{1,2,0:T(8,128)S(1)} custom-call(f32[8,128,128]{2,1,0:T(8,128)S(1)} %get-tuple-element.12), custom_call_target="InvertDiagBlocksLowerTriangular" | custom-call | tf_op jit(solution)/shard_map/triangular_solve | solution.py:26
  561.7 2.7 constant_dynamic-update-slice_fusion.17
  564.5 2.5 convolution_subtract_fusion.4
  568.3 2.3 convolution_subtract_fusion.3
  571.9 3.1 fusion.23
  575.0 2.3 constant_dynamic-update-slice_fusion.14
  577.3 5.2 fusion.26
  582.5 2.4 constant_dynamic-update-slice_fusion.13
  584.9 4.3 convolution_subtract_fusion.2
  590.4 4.6 convolution_subtract_fusion
  596.1 5.7 convolution_subtract_fusion.1
  606.1 38.4 %all-reduce.1 = (f32[1024]{0:T(1024)S(1)}, f32[1024]{0:T(1024)S(1)}) all-reduce(f32[1024]{0:T(1024)S(1)} %get-tuple-element.14, f32[1024]{0:T(1024)S(1)} %get-tuple-element.13), channel_id=1, replica_groups=mesh['grp'=4,'dev'=8] {'grp','dev'}, use_global_device_ids=true, to_apply=%region_22.23 | all-reduce | flops 2048 | bytes 16384 | tf_op jit(solution)/shard_map/psum | solution.py:28
  644.5 5.3 divide_convert_fusion
  649.9 6.4 copy.22
  (86 shorter events, 51.1 us)
Async XLA Ops:
  6.5 7.5 %copy-start.1 = (bf16[2048,256]{1,0:T(8,128)(2,1)S(1)}, bf16[2048,256]{1,0:T(8,128)(2,1)}, u32[]{:S(2)}) copy-start(bf16[2048,256]{1,0:T(8,128)(2,1)} %param.3) | copy-start | bytes 3145732
  6.5 204.6 %all-gather.2.cloned.1.call-start = ((), (), s32[]{:S(2)}) async-start(), calls=%async_computation | async-start | bytes 34603008 | tf_op jit(solution)/shard_map/all_gather | solution.py:22
  234.3 5.4 copy-start.5
  245.7 2.0 copy-start.2
  561.7 5.3 copy-start.3
  561.7 6.6 slice-start
  564.5 3.8 slice-start.1
  568.3 2.3 copy-start.4
  602.9 3.2 copy-start
Sparse Core Ops, SparseCore 0:
  14.2 196.8 all-gather.1
